TPU v7x, 32 devices: a whole 2x2x4 slice. The times are simulated.
32 devices in a mesh: rep: 4 (over z), row: 4 (over x, core), col: 2 (over y).
Axes of the slice: x: 2, y: 2, z: 4, core: 2. Of those that a mesh axis runs over, the one named last changes fastest.
Arguments:
- grad_parts: bfloat16 [4, 16384, 6144], P('rep', ('row', 'col')), may hold values from -0.03125 to 0.03125, as said below
- statistic: float32 [6144, 6144], P('row', 'col'), may hold values from -150 to 150, as said below
Outputs:
- gram_matrix: float32 [6144, 6144], P('row', 'col')
- statistic_next: float32 [6144, 6144], P('row', 'col')
Inputs may be any that keep to these rules, and one draw needn't show every extreme that they name: Every entry of grad_parts has a magnitude between 2^-10 and 2^-5. statistic is symmetric and positive definite.
All inputs are finite; a program needn't handle non-finite values.
Results may differ from a plain program's by a relative error of at most 0.008.
Values may be sent and summed in bfloat16 or wider, within the bound.
A program may use at most 192 MiB of HBM per device.

v0:
```python
import jax
import jax.numpy as jnp
from jax import lax
from jax.sharding import PartitionSpec as P


def shards(grad_parts, statistic):
    own_part = grad_parts[0].astype(jnp.float32)
    summed = lax.psum_scatter(own_part.astype(jnp.bfloat16), "rep", scatter_dimension=0, tiled=True)
    rows_panel = lax.all_to_all(summed, "row", split_axis=1, concat_axis=0, tiled=True)
    cols_panel = lax.all_to_all(summed, "col", split_axis=1, concat_axis=0, tiled=True)
    row_count = lax.axis_size("row")
    col_count = lax.axis_size("col")
    quarter = summed.shape[0]
    left_whole = lax.all_gather(rows_panel, "col", axis=0, tiled=True)
    left_order = (
        left_whole.reshape(col_count, row_count, quarter, -1)
        .transpose(1, 0, 2, 3)
        .reshape(row_count * col_count * quarter, -1)
    )
    partial_tile = lax.dot_general(
        left_order,
        lax.all_gather(cols_panel, "row", axis=0, tiled=True),
        (((0,), (0,)), ((), ())),
        preferred_element_type=jnp.float32,
    )
    gram_tile = lax.psum(partial_tile, "rep")
    return (gram_tile, 0.95 * statistic + 0.05 * gram_tile)


def solution(mesh):
    return jax.shard_map(
        shards,
        mesh=mesh,
        in_specs=(P("rep", ("row", "col"), None), P("row", "col")),
        out_specs=(P("row", "col"), P("row", "col")),
        check_vma=False,
    )
```

profile of v0, /device:TPU:0, one launch (start us, length us, event | category | flops | bytes accessed | tf_op | source)
XLA Modules:
  0.0 1626.5 jit_solution(12246390620208611394)
XLA Ops:
  7.2 0.0 reduce-scatter.2.cloned.1.call-start
  7.2 30.3 %copy.5 = bf16[1,2048,6144]{1,2,0:T(8,128)(2,1)} copy(bf16[1,2048,6144]{2,1,0:T(8,128)(2,1)} %param.2) | data formatting | bytes 50331648 | tf_op args[0]
  37.5 0.0 reduce-scatter.2.cloned.1.call-update
  37.6 0.0 all-gather.3.cloned.1.call-start
  37.6 417.0 %reduce-scatter.2.cloned.1.call-done = bf16[512,6144]{0,1:T(8,128)(2,1)} async-done(((bf16[2048,6144]{0,1:T(8,128)(2,1)}), bf16[512,6144]{0,1:T(8,128)(2,1)}) %reduce-scatter.2.cloned.1.call-update) | async-done | bytes 6291472 | tf_op jit(solution)/shard_map/reduce_scatter | solution.py:9
  454.7 77.3 %all_to_all.38 = bf16[512,4,1536]{0,2,1:T(8,128)(2,1)} all-to-all(bf16[512,4,1536]{0,2,1:T(8,128)(2,1)} %bitcast.15), channel_id=1, replica_groups=mesh['rep'=4,'row'=4,'col'=2] {'row'}, dimensions={1} | all-to-all | bytes 12582912 | tf_op jit(solution)/shard_map/all_to_all | solution.py:10
  532.0 8.6 copy.6
  540.6 0.0 all-gather.3.cloned.1.call-update
  540.6 0.0 all-gather.5.cloned.1.call-start
  540.7 140.8 %all_to_all.39 = bf16[512,2,3072]{0,2,1:T(8,128)(2,1)} all-to-all(bf16[512,2,3072]{0,2,1:T(8,128)(2,1)} %bitcast.16), channel_id=1, replica_groups=mesh['rep'=4,'row'=4,'col'=2] {'col'}, dimensions={1} | all-to-all | bytes 12582912 | tf_op jit(solution)/shard_map/all_to_all | solution.py:11
  681.4 8.6 copy.8
  690.1 0.0 all-gather.5.cloned.1.call-update
  690.1 0.0 all-reduce.2.cloned.1.call-start
  690.2 64.5 %all-gather.3.cloned.1.call-done = bf16[4096,1536]{1,0:T(8,128)(2,1)} async-done(((bf16[2048,1536]{1,0:T(8,128)(2,1)}), bf16[4096,1536]{1,0:T(8,128)(2,1)}) %all-gather.3.cloned.1.call-update) | async-done | bytes 12582928 | tf_op jit(solution)/shard_map/all_gather | solution.py:15
  754.7 11.1 copy.7
  765.8 145.7 %all-gather.5.cloned.1.call-done = bf16[4096,3072]{1,0:T(8,128)(2,1)} async-done(((bf16[1024,3072]{1,0:T(8,128)(2,1)}), bf16[4096,3072]{1,0:T(8,128)(2,1)}) %all-gather.5.cloned.1.call-update) | async-done | bytes 25165840 | tf_op jit(solution)/shard_map/all_gather | solution.py:23
  911.5 48.0 %fusion = f32[1536,3072]{1,0:T(8,128)} fusion(bf16[4096,1536]{1,0:T(8,128)(2,1)} %bitcast.21, bf16[4096,3072]{1,0:T(8,128)(2,1)} %all-gather.5.cloned.1.call-done), kind=kOutput, calls=%fused_computation.1 | convolution fusion | flops 38654705664 | bytes 56623104 | tf_op jit(solution)/shard_map/dot_general | solution.py:21
  959.5 0.0 all-reduce.2.cloned.1.call-update
  959.6 629.5 %all-reduce.2.cloned.1.call-done = f32[1536,3072]{1,0:T(8,128)} async-done(((f32[1536,3072]{1,0:T(8,128)}), f32[1536,3072]{1,0:T(8,128)}) %all-reduce.2.cloned.1.call-update) | async-done | bytes 18874384 | tf_op jit(solution)/shard_map/psum | solution.py:27
  1589.1 0.0 copy-start
  1589.1 20.7 %multiply_add_fusion = f32[1536,3072]{1,0:T(8,128)} fusion(f32[1536,3072]{1,0:T(8,128)} %all-reduce.2.cloned.1.call-done, f32[1536,3072]{1,0:T(8,128)} %param.3), kind=kLoop, calls=%fused_computation | loop fusion | flops 14155776 | bytes 56623104 | tf_op jit(solution)/shard_map/add | solution.py:28
  1609.8 3.3 copy-done
  1613.1 6.8 copy.10
Async XLA Ops:
  7.2 447.5 %reduce-scatter.2.cloned.1.call-start = ((), (), s32[]{:S(2)}) async-start(), calls=%async_computation.3 | async-start | bytes 31457280 | tf_op jit(solution)/shard_map/reduce_scatter | solution.py:9
  37.6 717.1 %all-gather.3.cloned.1.call-start = ((), (), s32[]{:S(2)}) async-start(), calls=%async_computation.4 | async-start | bytes 18874368 | tf_op jit(solution)/shard_map/all_gather | solution.py:15
  540.6 370.9 %all-gather.5.cloned.1.call-start = ((), (), s32[]{:S(2)}) async-start(), calls=%async_computation.5 | async-start | bytes 31457280 | tf_op jit(solution)/shard_map/all_gather | solution.py:23
  690.1 899.0 %all-reduce.2.cloned.1.call-start = ((), (), s32[]{:S(2)}) async-start(), calls=%async_computation.6 | async-start | bytes 37748736 | tf_op jit(solution)/shard_map/psum | solution.py:27
  1589.1 24.0 %copy-start = (f32[1536,3072]{1,0:T(8,128)S(1)}, f32[1536,3072]{1,0:T(8,128)}, u32[]{:S(2)}) copy-start(f32[1536,3072]{1,0:T(8,128)} %all-reduce.2.cloned.1.call-done) | copy-start | bytes 56623108
Sparse Core Ops, SparseCore 0:
  37.7 416.9 reduce-scatter.1
  540.7 213.8 all-gather.2
  756.2 155.2 all-gather.4
  959.7 629.3 all-reduce.1
where the time goes:
time: 1630 us
  waiting for transfers between devices  1260 us (77%)
  blocking collectives  218 us (13%)
  local copies, waits for them, and re-layouts  68.9 us (4%)
  matrix products  48 us (3%)
  other arithmetic  20.7 us (1%)
    psum x1, waiting for transfers between devices, shards(): gram_tile = lax.psum(partial_tile, 'rep')  630 us
    reduce_scatter x1, waiting for transfers between devices, shards(): lax.psum_scatter(own_part.astype(jnp.bfloat16), 'rep', scatter_dimension=...  417 us
    all_gather x1, waiting for transfers between devices, shards(): lax.all_gather(cols_panel, 'row', axis=0, tiled=True)  146 us
    all_to_all x1, blocking collectives, shards(): lax.all_to_all(summed, 'col', split_axis=1, concat_axis=0, tiled=True)  141 us
    all_to_all x1, blocking collectives, shards(): lax.all_to_all(summed, 'row', split_axis=1, concat_axis=0, tiled=True)  77.3 us
    all_gather x1, waiting for transfers between devices, shards(): left_whole = lax.all_gather(rows_panel, 'col', axis=0, tiled=True)  64.5 us
    dot_general x1, matrix products, shards(): lax.dot_general(left_order, lax.all_gather(cols_panel, 'row', axis=0, til...  48 us
    unnamed x4, local copies, waits for them, and re-layouts  40.5 us
  transfers between devices with their start and end apart: 4, of which 4 were waited for; matrix products, arithmetic and copies ran while one was open for 1% of the time, Pallas kernels for 0%

commit v1 on v0

--- a/solution.py
+++ b/solution.py
@@ -2,6 +2,8 @@
 import jax.numpy as jnp
 from jax import lax
 from jax.sharding import PartitionSpec as P
+
+solve_points = lambda sheet, axis_tag: lax.all_gather(sheet, axis_tag).sum(axis=0)
 
 
 def shards(grad_parts, statistic):
@@ -24,7 +26,7 @@
         (((0,), (0,)), ((), ())),
         preferred_element_type=jnp.float32,
     )
-    gram_tile = lax.psum(partial_tile, "rep")
+    gram_tile = solve_points(partial_tile, "rep")
     return (gram_tile, 0.95 * statistic + 0.05 * gram_tile)
 
 

time: 1630 us -> 2270 us (1.39)
  waiting for transfers between devices: 1260 us -> 1880 us
  other arithmetic: 20.7 us -> 52 us
    all_gather x0 -> x1, waiting for transfers between devices: none -> 1250 us  [lax.all_gather(sheet, axis_tag).sum(axis=0)]
    psum x1 -> x0, waiting for transfers between devices: 630 us -> none  [shards(): gram_tile = lax.psum(partial_tile, 'rep')]
    reduce_sum x0 -> x1, other arithmetic: none -> 31.5 us  [lax.all_gather(sheet, axis_tag).sum(axis=0)]
where the time goes in v1:
time: 2270 us
  waiting for transfers between devices  1880 us (83%)
  blocking collectives  218 us (10%)
  local copies, waits for them, and re-layouts  59.2 us (3%)
  other arithmetic  52 us (2%)
  matrix products  48 us (2%)
    all_gather x1, waiting for transfers between devices, lax.all_gather(sheet, axis_tag).sum(axis=0)  1250 us
    reduce_scatter x1, waiting for transfers between devices, shards(): lax.psum_scatter(own_part.astype(jnp.bfloat16), 'rep', scatter_dimension=...  417 us
    all_gather x1, waiting for transfers between devices, shards(): lax.all_gather(cols_panel, 'row', axis=0, tiled=True)  146 us
    all_to_all x1, blocking collectives, shards(): lax.all_to_all(summed, 'col', split_axis=1, concat_axis=0, tiled=True)  141 us
    all_to_all x1, blocking collectives, shards(): lax.all_to_all(summed, 'row', split_axis=1, concat_axis=0, tiled=True)  77.3 us
    all_gather x1, waiting for transfers between devices, shards(): left_whole = lax.all_gather(rows_panel, 'col', axis=0, tiled=True)  64.5 us
    dot_general x1, matrix products, shards(): lax.dot_general(left_order, lax.all_gather(cols_panel, 'row', axis=0, til...  48 us
  transfers between devices with their start and end apart: 4, of which 4 were waited for; matrix products, arithmetic and copies ran while one was open for 1% of the time, Pallas kernels for 0%

profile of v1, /device:TPU:0, one launch (start us, length us, event | category | flops | bytes accessed | tf_op | source)
XLA Modules:
  0.0 2267.7 jit_solution(1987859502365859458)
XLA Ops:
  7.2 0.0 reduce-scatter.2.cloned.1.call-start
  7.2 30.8 %copy.5 = bf16[1,2048,6144]{1,2,0:T(8,128)(2,1)} copy(bf16[1,2048,6144]{2,1,0:T(8,128)(2,1)} %param.2) | data formatting | bytes 50331648 | tf_op args[0]
  38.0 0.0 reduce-scatter.2.cloned.1.call-update
  38.0 0.0 all-gather.5.cloned.1.call-start
  38.1 417.0 %reduce-scatter.2.cloned.1.call-done = bf16[512,6144]{0,1:T(8,128)(2,1)} async-done(((bf16[2048,6144]{0,1:T(8,128)(2,1)}), bf16[512,6144]{0,1:T(8,128)(2,1)}) %reduce-scatter.2.cloned.1.call-update) | async-done | bytes 6291472 | tf_op jit(solution)/shard_map/reduce_scatter | solution.py:11
  455.1 77.3 %all_to_all.38 = bf16[512,4,1536]{0,2,1:T(8,128)(2,1)} all-to-all(bf16[512,4,1536]{0,2,1:T(8,128)(2,1)} %bitcast.16), channel_id=1, replica_groups=mesh['rep'=4,'row'=4,'col'=2] {'row'}, dimensions={1} | all-to-all | bytes 12582912 | tf_op jit(solution)/shard_map/all_to_all | solution.py:12
  532.4 8.6 copy.6
  541.0 0.0 all-gather.5.cloned.1.call-update
  541.1 0.0 all-gather.7.cloned.1.call-start
  541.1 140.7 %all_to_all.39 = bf16[512,2,3072]{0,2,1:T(8,128)(2,1)} all-to-all(bf16[512,2,3072]{0,2,1:T(8,128)(2,1)} %bitcast.17), channel_id=1, replica_groups=mesh['rep'=4,'row'=4,'col'=2] {'col'}, dimensions={1} | all-to-all | bytes 12582912 | tf_op jit(solution)/shard_map/all_to_all | solution.py:13
  681.9 8.7 copy.8
  690.5 0.0 all-gather.7.cloned.1.call-update
  690.5 0.0 all-gather.9.cloned.1.call-start
  690.6 64.5 %all-gather.5.cloned.1.call-done = bf16[4096,1536]{1,0:T(8,128)(2,1)} async-done(((bf16[2048,1536]{1,0:T(8,128)(2,1)}), bf16[4096,1536]{1,0:T(8,128)(2,1)}) %all-gather.5.cloned.1.call-update) | async-done | bytes 12582928 | tf_op jit(solution)/shard_map/all_gather | solution.py:17
  755.1 11.1 copy.7
  766.2 145.7 %all-gather.7.cloned.1.call-done = bf16[4096,3072]{1,0:T(8,128)(2,1)} async-done(((bf16[1024,3072]{1,0:T(8,128)(2,1)}), bf16[4096,3072]{1,0:T(8,128)(2,1)}) %all-gather.7.cloned.1.call-update) | async-done | bytes 25165840 | tf_op jit(solution)/shard_map/all_gather | solution.py:25
  911.9 48.0 %fusion = f32[1536,3072]{1,0:T(8,128)} fusion(bf16[4096,1536]{1,0:T(8,128)(2,1)} %bitcast.22, bf16[4096,3072]{1,0:T(8,128)(2,1)} %all-gather.7.cloned.1.call-done), kind=kOutput, calls=%fused_computation.1 | convolution fusion | flops 38654705664 | bytes 56623104 | tf_op jit(solution)/shard_map/dot_general | solution.py:23
  960.0 0.0 all-gather.9.cloned.1.call-update
  960.0 1249.2 %all-gather.9.cloned.1.call-done = f32[6144,3072]{1,0:T(8,128)} async-done(((f32[1536,3072]{1,0:T(8,128)}), f32[6144,3072]{1,0:T(8,128)}) %all-gather.9.cloned.1.call-update) | async-done | bytes 75497488 | tf_op jit(solution)/shard_map/all_gather | solution.py:6
  2209.2 31.5 %reduce_sum.9 = f32[1536,3072]{1,0:T(8,128)} reduce(f32[4,1536,3072]{2,1,0:T(8,128)} %bitcast.10, f32[]{:T(128)} %constant.0.clone.1), dimensions={0}, to_apply=%region_1.0 | reduce | flops 14155776 | bytes 94371840 | tf_op jit(solution)/shard_map/reduce_sum | solution.py:6
  2240.7 20.5 multiply_add_fusion
Async XLA Ops:
  7.2 447.9 %reduce-scatter.2.cloned.1.call-start = ((), (), s32[]{:S(2)}) async-start(), calls=%async_computation.3 | async-start | bytes 31457280 | tf_op jit(solution)/shard_map/reduce_scatter | solution.py:11
  38.0 717.1 %all-gather.5.cloned.1.call-start = ((), (), s32[]{:S(2)}) async-start(), calls=%async_computation.4 | async-start | bytes 18874368 | tf_op jit(solution)/shard_map/all_gather | solution.py:17
  541.1 370.9 %all-gather.7.cloned.1.call-start = ((), (), s32[]{:S(2)}) async-start(), calls=%async_computation.5 | async-start | bytes 31457280 | tf_op jit(solution)/shard_map/all_gather | solution.py:25
  690.5 1518.6 %all-gather.9.cloned.1.call-start = ((), (), s32[]{:S(2)}) async-start(), calls=%async_computation.6 | async-start | bytes 94371840 | tf_op jit(solution)/shard_map/all_gather | solution.py:6
Sparse Core Ops, SparseCore 0:
  38.1 416.9 reduce-scatter.1
  541.2 213.8 all-gather.4
  756.7 155.2 all-gather.6
  960.1 1248.9 all-gather.8
